TPU v7x, 32 devices: a whole 2x2x4 slice. The times are simulated.
32 devices in a mesh: group: 2 (over x), lon: 16 (over z, y, core).
Axes of the slice: x: 2, y: 2, z: 4, core: 2. Of those that a mesh axis runs over, the one named last changes fastest.
Arguments:
- initial_state: bfloat16 [512, 8, 64, 128], P('lon', 'group'), parts along dimension 1, may hold values from -10 to 10
- self_weight: bfloat16 [128, 128], replicated, may hold values from -0.5 to 0.5
- neighbour_weight: bfloat16 [6, 128, 128], replicated, may hold values from -0.5 to 0.5
- edge_bias: float32 [6, 128], replicated, may hold values from -4 to 4
- message_weight: bfloat16 [128, 128], replicated, may hold values from -0.5 to 0.5
- state_weight: bfloat16 [128, 128], replicated, may hold values from -0.375 to 0.375
- inbound_weight: bfloat16 [128, 128], replicated, may hold values from -0.375 to 0.375
- node_bias: float32 [128], replicated, may hold values from -2.5 to 2.5
- output_weight: bfloat16 [128, 128], replicated, may hold values from -0.5 to 0.5
- node_gain: float32 [128], replicated, may hold values from 0.5 to 1.5
Outputs:
- final_state: bfloat16 [512, 8, 64, 128], P('lon', 'group'), parts along dimension 1
- profiles: float32 [8, 64, 128], P('group'), parts along dimension 0
There are 2 independent parts, one for each index of `group`. A program takes and returns all parts, laid end to end along the dimension named above; an argument that names none is the same for every part. Nothing has to cross between parts.
All inputs are finite; a program needn't handle non-finite values.
Results may differ from a plain program's by a relative error of at most 0.0095.
Values may be sent and summed in bfloat16 or wider, within the bound.
A program may use at most 128 MiB of HBM per device.

v0:
```python
import functools
import math

import jax
import jax.numpy as jnp
from jax import lax
from jax.experimental import pallas as pl
from jax.experimental.pallas import tpu as pltpu
from jax.sharding import PartitionSpec as P

STEPS = 4
SUB = 16
CHUNK = 8
COLS = 4
PER_DOT = 4
PER_DOT_NODE = 4
F32 = jnp.float32
BF16 = jnp.bfloat16


def latitude_weights(rows):
    return [math.cos(-math.pi / 2 + (j + 0.5) * (math.pi / rows)) for j in range(rows)]


def dot(a, b):
    return jnp.dot(a, b, preferred_element_type=F32)


def kernel(
    devices,
    state_in,
    self_weight,
    neighbour_weight,
    edge_bias,
    message_weight,
    state_weight,
    inbound_weight,
    node_bias,
    output_weight,
    node_gain,
    state_out,
    profiles,
    raw,
    wide,
    ext,
    mean,
    halo,
    carry,
    total_bias,
    inverse,
    w_pair,
    w_hidden,
    w_out,
    w_ones,
    table,
    acc,
    part,
    gathered,
    combined,
    in_sem,
    out_sem,
    halo_send,
    halo_recv,
    rs_send,
    rs_recv,
    ag_send,
    ag_recv,
):
    columns, rows, levels, width = raw.shape
    tiles = levels // SUB
    area = rows * levels
    groups = columns // COLS
    chunks = levels // CHUNK
    copies = devices // chunks
    me = lax.axis_index("lon")
    right, left = lax.rem(me + 1, devices), lax.rem(me + devices - 1, devices)
    mine, which = me // copies, lax.rem(me, copies)
    weights = latitude_weights(rows)
    scale = 1.0 / (columns * devices * sum(weights))

    def peer(offset):
        return lax.rem(me + offset, devices)

    barrier = pltpu.get_barrier_semaphore()
    for offset in range(1, devices):
        pl.semaphore_signal(barrier, inc=1, device_id={"lon": peer(offset)})

    def load(group):
        span = pl.ds(group * COLS, COLS)
        return pltpu.make_async_copy(state_in.at[span], raw.at[span], in_sem.at[group])

    def unload(group):
        span = pl.ds(group * COLS, COLS)
        return pltpu.make_async_copy(raw.at[span], state_out.at[span], out_sem.at[group])

    def order(k):
        return lax.rem(k + groups - 1, groups)

    @pl.loop(0, groups)
    def _(k):
        load(order(k)).start()

    self_w = self_weight[...]
    for pair in range(3):
        w_pair[pair, :width, :width] = self_w
        w_pair[pair, width:, width:] = self_w
        w_pair[pair, width:, :width] = neighbour_weight[2 * pair]
        w_pair[pair, :width, width:] = neighbour_weight[2 * pair + 1]
    w_hidden[:width] = state_weight[...]
    w_hidden[width:] = dot(message_weight[...], inbound_weight[...]).astype(BF16)
    out_w = output_weight[...].astype(F32)
    out_w = (out_w - jnp.mean(out_w, axis=1, keepdims=True)).astype(BF16)
    w_out[...] = jnp.zeros_like(w_out)
    w_out[:width, :width] = out_w
    w_out[width:, width:] = out_w
    w_ones[...] = jnp.zeros_like(w_ones)
    w_ones[:width, :width] = jnp.full((width, width), 1.0 / width, BF16)
    w_ones[width:, width:] = jnp.full((width, width), 1.0 / width, BF16)
    sub = lax.broadcasted_iota(jnp.int32, (SUB, width), 0)
    for j in range(rows):
        for k in range(tiles):
            count = jnp.full((SUB, width), 2.0 + (j < rows - 1) + (j > 0), F32)
            bias = jnp.broadcast_to(edge_bias[0:1] + edge_bias[1:2], (SUB, width))
            if j < rows - 1:
                bias = bias + edge_bias[2:3]
            if j > 0:
                bias = bias + edge_bias[3:4]
            up = jnp.ones((SUB, width), F32)
            down = up
            if k == tiles - 1:
                up = (sub < SUB - 1).astype(F32)
            if k == 0:
                down = (sub > 0).astype(F32)
            total_bias[j, k] = bias + up * edge_bias[4:5] + down * edge_bias[5:6]
            inverse[j, k] = 1.0 / (count + up + down)

    def halo_copies(t):
        return (
            pltpu.make_async_remote_copy(
                src_ref=ext.at[columns],
                dst_ref=halo.at[t, 0],
                send_sem=halo_send.at[t, 0],
                recv_sem=halo_recv.at[t, 0],
                device_id={"lon": right},
            ),
            pltpu.make_async_remote_copy(
                src_ref=ext.at[1],
                dst_ref=halo.at[t, 1],
                send_sem=halo_send.at[t, 1],
                recv_sem=halo_recv.at[t, 1],
                device_id={"lon": left},
            ),
        )

    def start_halo(t):
        for copy in halo_copies(t):
            copy.start()

    def scatter(t, target, source):
        return pltpu.make_async_remote_copy(
            src_ref=part.at[t, target // copies],
            dst_ref=gathered.at[t, source],
            send_sem=rs_send.at[t, target],
            recv_sem=rs_recv.at[t, source],
            device_id={"lon": target},
        )

    def start_scatter(t):
        part[t] = acc[...].reshape(chunks, CHUNK, width)

        @pl.loop(1, devices)
        def _(offset):
            scatter(t, peer(offset), me).start()

    def spread(t, target, source):
        return pltpu.make_async_remote_copy(
            src_ref=combined.at[t, source],
            dst_ref=combined.at[t, source],
            send_sem=ag_send.at[t, target],
            recv_sem=ag_recv.at[t, source],
            device_id={"lon": target * copies + which},
        )

    def combine(t):
        gathered[t, me] = part[t, mine]

        @pl.loop(1, devices)
        def _(offset):
            scatter(t, peer(offset), peer(offset)).wait_recv()

        total = gathered[t, 0]
        for source in range(1, devices):
            total = total + gathered[t, source]
        combined[t, mine] = total * scale

        @pl.loop(1, chunks)
        def _(offset):
            spread(t, lax.rem(mine + offset, chunks), mine).start()

    def finish(t):
        @pl.loop(1, chunks)
        def _(offset):
            other = lax.rem(mine + offset, chunks)
            spread(t, other, other).wait_recv()

        profile = combined[t].reshape(levels, width)
        high = profile.astype(BF16)
        low = (profile - high.astype(F32)).astype(BF16)
        shift = dot(high, state_weight[...]) + dot(low, state_weight[...])
        table[...] = node_bias[...] - shift
        tiled = profile.reshape(tiles, SUB, width)
        for k in range(tiles):
            profiles[t, pl.ds(k, SUB, stride=tiles), :] = tiled[k]

        @pl.loop(1, devices)
        def _(offset):
            scatter(t, peer(offset), me).wait_send()

        @pl.loop(1, chunks)
        def _(offset):
            spread(t, lax.rem(mine + offset, chunks), mine).wait_send()

    def accumulate(fresh):
        for j in range(rows):
            line = fresh[0, j]
            for i in range(1, fresh.shape[0]):
                line = line + fresh[i, j]
            line = line * weights[j]
            added = line if j == 0 else added + line
        acc[...] += added

    acc[...] = jnp.zeros_like(acc)

    @pl.loop(0, groups)
    def _(k):
        group = order(k)
        base = group * COLS
        load(group).wait()

        @pl.when(k == 2)
        def _():
            pl.semaphore_wait(barrier, devices - 1)
            start_halo(0)

        block = raw[pl.ds(base, COLS)].astype(F32).reshape(COLS * rows, levels, width)
        wide[...] = block
        accumulate(
            jnp.concatenate(
                [wide[:, pl.ds(k, SUB, stride=tiles), :] for k in range(tiles)], axis=1
            ).reshape(COLS, rows, levels, width)
        )
        for k in range(tiles):
            piece = wide[:, pl.ds(k, SUB, stride=tiles), :].astype(BF16)
            ext[pl.ds(base + 1, COLS), :, k] = piece.reshape(COLS, rows, SUB, width)

    start_scatter(0)

    def lifted(x, index):
        return jnp.maximum(x, -edge_bias[index : index + 1])

    def edges(t):
        for copy in halo_copies(t):
            copy.wait_recv()
        ext[0] = halo[t, 0]
        ext[columns + 1] = halo[t, 1]
        both = jnp.concatenate([ext[0].reshape(area, width), ext[1].reshape(area, width)], axis=1)
        carry[...] = lifted(dot(both, w_pair[0, :, width:]), 1).reshape(rows, levels, width)

        @pl.loop(0, groups)
        def _(group):
            @pl.when(group == groups // 2)
            def _():
                combine(t)

            for piece in range(COLS // PER_DOT):
                edge_piece(group * COLS + piece * PER_DOT)

        for copy in halo_copies(t):
            copy.wait_send()

    def edge_piece(base):
        n = PER_DOT
        here = ext[pl.ds(base + 1, n)]
        flat = here.reshape(n * area, width)
        ahead = ext[pl.ds(base + 2, n)].reshape(n * area, width)
        x = dot(jnp.concatenate([flat, ahead], axis=1), w_pair[0])
        east = lifted(x[:, :width], 0).reshape(n, rows, levels, width)
        west = lifted(x[:, width:], 1).reshape(n, rows, levels, width)
        west = jnp.concatenate([carry[...][None], west], axis=0)
        carry[...] = west[n]
        longitude = east + west[:n]

        lower = here[:, :-1].reshape(n * (area - levels), width)
        upper = here[:, 1:].reshape(n * (area - levels), width)
        x = dot(jnp.concatenate([lower, upper], axis=1), w_pair[1])
        north = lifted(x[:, :width], 2).reshape(n, rows - 1, levels, width)
        south = lifted(x[:, width:], 3).reshape(n, rows - 1, levels, width)

        tile = here.reshape(n * rows, tiles, SUB, width)
        first = tile[:, 0].astype(F32)
        first = pltpu.roll(first, SUB - 1, 1).astype(BF16).reshape(n * rows, 1, SUB, width)
        above = jnp.concatenate([tile[:, 1:], first], axis=1).reshape(n * area, width)
        x = dot(jnp.concatenate([flat, above], axis=1), w_pair[2])
        up = lifted(x[:, :width], 4).reshape(n * rows, tiles, SUB, width)
        down = lifted(x[:, width:], 5).reshape(n * rows, tiles, SUB, width)
        row = lax.broadcasted_iota(jnp.int32, (1, SUB, width), 1)
        last = jnp.where(row < SUB - 1, up[:, tiles - 1], 0.0)
        wrapped = jnp.where(row > 0, pltpu.roll(down[:, tiles - 1], 1, 1), 0.0)
        for k in range(tiles):
            r = (up[:, k] if k < tiles - 1 else last) + (down[:, k - 1] if k > 0 else wrapped)
            r = r.reshape(n, rows, SUB, width)
            span = slice(k * SUB, (k + 1) * SUB)
            for j in range(rows):
                s = longitude[:, j, span] + r[:, j]
                if j < rows - 1:
                    s = s + north[:, j, span]
                if j > 0:
                    s = s + south[:, j - 1, span]
                s = (s + total_bias[j, k]) * inverse[j, k]
                mean[pl.ds(base, n), j, k] = s.astype(BF16)

    def nodes(t, last):
        acc[...] = jnp.zeros_like(acc)

        @pl.loop(0, groups)
        def _(k):
            if not last:

                @pl.when(k == 2)
                def _():
                    start_halo(t + 1)

            group = order(k)
            for piece in range(COLS // PER_DOT_NODE):
                node_piece(group * COLS + piece * PER_DOT_NODE, last)
            if last:
                unload(group).start()

        if not last:
            start_scatter(t + 1)

    def node_piece(base, last):
        n = PER_DOT_NODE
        size = n * area
        here = ext[pl.ds(base + 1, n)].reshape(size, width)
        inbound = mean[pl.ds(base, n)].reshape(size, width)
        hidden = dot(jnp.concatenate([here, inbound], axis=1), w_hidden[...])
        hidden = hidden.reshape(n * rows, levels, width) + table[...]
        hidden = jnp.maximum(hidden, 0.0).astype(BF16).reshape(size, width)
        half = size // 2
        out = dot(jnp.concatenate([hidden[:half], hidden[half:]], axis=1), w_out[...])
        spread_ = dot((out * out).astype(BF16), w_ones[...])
        factor = lax.rsqrt(spread_ + 1e-05)
        gain = node_gain[...]
        gain = jnp.concatenate([gain, gain], axis=1)
        update = out * factor * gain
        update = jnp.concatenate([update[:, :width], update[:, width:]], axis=0)
        fresh = here.astype(F32) + update
        if last:
            tiled = fresh.reshape(n * rows, tiles, SUB, width)
            for k in range(tiles):
                wide[: n * rows, pl.ds(k, SUB, stride=tiles), :] = tiled[:, k]
            whole = wide[: n * rows].astype(BF16)
            raw[pl.ds(base, n)] = whole.reshape(n, rows, levels, width)
        else:
            ext[pl.ds(base + 1, n)] = fresh.astype(BF16).reshape(n, rows, tiles, SUB, width)
            accumulate(fresh.reshape(n, rows, levels, width))

    @pl.loop(0, STEPS - 1)
    def _(t):
        edges(t)
        finish(t)
        nodes(t, False)

    edges(STEPS - 1)
    finish(STEPS - 1)
    nodes(STEPS - 1, True)

    @pl.loop(0, groups)
    def _(group):
        unload(group).wait()


def body(
    initial_state,
    self_weight,
    neighbour_weight,
    edge_bias,
    message_weight,
    state_weight,
    inbound_weight,
    node_bias,
    output_weight,
    node_gain,
):
    columns, rows, levels, width = initial_state.shape
    devices = lax.axis_size("lon")
    tiles = levels // SUB
    groups = columns // COLS
    chunks = levels // CHUNK
    vmem = pl.BlockSpec(memory_space=pltpu.VMEM)
    hbm = pl.BlockSpec(memory_space=pl.ANY)
    dma = pltpu.SemaphoreType.DMA
    return pl.pallas_call(
        functools.partial(kernel, devices),
        out_shape=(
            jax.ShapeDtypeStruct(initial_state.shape, BF16),
            jax.ShapeDtypeStruct((STEPS, levels, width), F32),
        ),
        in_specs=[hbm] + [vmem] * 9,
        out_specs=(hbm, vmem),
        scratch_shapes=[
            pltpu.VMEM((columns, rows, levels, width), BF16),
            pltpu.VMEM((COLS * rows, levels, width), F32),
            pltpu.VMEM((columns + 2, rows, tiles, SUB, width), BF16),
            pltpu.VMEM((columns, rows, tiles, SUB, width), BF16),
            pltpu.VMEM((STEPS, 2, rows, tiles, SUB, width), BF16),
            pltpu.VMEM((rows, levels, width), F32),
            pltpu.VMEM((rows, tiles, SUB, width), F32),
            pltpu.VMEM((rows, tiles, SUB, width), F32),
            pltpu.VMEM((3, 2 * width, 2 * width), BF16),
            pltpu.VMEM((2 * width, width), BF16),
            pltpu.VMEM((2 * width, 2 * width), BF16),
            pltpu.VMEM((2 * width, 2 * width), BF16),
            pltpu.VMEM((levels, width), F32),
            pltpu.VMEM((levels, width), F32),
            pltpu.VMEM((STEPS, chunks, CHUNK, width), F32),
            pltpu.VMEM((STEPS, devices, CHUNK, width), F32),
            pltpu.VMEM((STEPS, chunks, CHUNK, width), F32),
            dma((groups,)),
            dma((groups,)),
            dma((STEPS, 2)),
            dma((STEPS, 2)),
            dma((STEPS, devices)),
            dma((STEPS, devices)),
            dma((STEPS, chunks)),
            dma((STEPS, chunks)),
        ],
        compiler_params=pltpu.CompilerParams(
            collective_id=0, has_side_effects=True, vmem_limit_bytes=60 * 1024 * 1024
        ),
    )(
        initial_state,
        self_weight,
        neighbour_weight,
        edge_bias,
        message_weight,
        state_weight,
        inbound_weight,
        node_bias.reshape(1, width),
        output_weight,
        node_gain.reshape(1, width),
    )


def solution(mesh):
    in_specs = (P("lon", "group", None, None), P(), P(), P(), P(), P(), P(), P(), P(), P())
    out_specs = (P("lon", "group", None, None), P("group", None, None))
    return jax.shard_map(body, mesh=mesh, in_specs=in_specs, out_specs=out_specs, check_vma=False)
```

profile of v0, /device:TPU:0, one launch (start us, length us, event | category | flops | bytes accessed | tf_op | source)
XLA Modules:
  0.0 74.6 jit_solution(17794294017286945048)
XLA Ops:
  0.6 70.1 %shard_map.113 = (bf16[32,4,64,128]{3,2,1,0:T(8,128)(2,1)}, f32[4,64,128]{2,1,0:T(8,128)}) custom-call(bf16[32,4,64,128]{3,2,1,0:T(8,128)(2,1)} %state_in.1, bf16[128,128]{1,0:T(8,128)(2,1)} %self_weight.1, bf16[6,128,128]{2,1,0:T(8,128)(2,1)} %neighbour_weight.1, f32[6,128]{1,0:T(8,128)} %edge_bias.1, bf16[128,128]{1,0:T(8,128)(2,1)} %message_weight.1, ...), custom_call_target="tpu_custom_call" | custom-call | tf_op jit(solution)/shard_map/pallas_call | solution.py:404
  70.7 0.0 copy-start
  70.7 3.2 %copy.14 = bf16[32,4,64,128]{3,2,1,0:T(8,128)(2,1)} copy(bf16[32,4,64,128]{3,2,1,0:T(8,128)(2,1)} %get-tuple-element.4) | data formatting | bytes 4194304
  74.0 0.0 copy-done
  74.0 0.7 copy.15
Async XLA Ops:
  70.7 3.2 %copy-start = (f32[4,64,128]{2,1,0:T(8,128)S(1)}, f32[4,64,128]{2,1,0:T(8,128)}, u32[]{:S(2)}) copy-start(f32[4,64,128]{2,1,0:T(8,128)} %get-tuple-element.5) | copy-start | bytes 393220
where the time goes:
time: 74.8 us; the launch traced here: 74.6 us
  Pallas kernels  70.1 us (94%)
  local copies, waits for them, and re-layouts  3.88 us (5%)
    pallas_call x1, Pallas kernels, body(): pl.pallas_call(functools.partial(kernel, devices), out_shape=(jax.ShapeDt...  70.1 us
    unnamed x4, local copies, waits for them, and re-layouts  3.88 us

commit v1 on v0

--- a/solution.py
+++ b/solution.py
@@ -10,8 +10,8 @@
 
 STEPS = 4
 SUB = 16
-CHUNK = 8
-COLS = 4
+INNER = 4
+COLS = 8
 PER_DOT = 4
 PER_DOT_NODE = 4
 F32 = jnp.float32
@@ -56,6 +56,7 @@
     acc,
     part,
     gathered,
+    outer,
     combined,
     in_sem,
     out_sem,
@@ -63,6 +64,8 @@
     halo_recv,
     rs_send,
     rs_recv,
+    ex_send,
+    ex_recv,
     ag_send,
     ag_recv,
 ):
@@ -70,11 +73,10 @@
     tiles = levels // SUB
     area = rows * levels
     groups = columns // COLS
-    chunks = levels // CHUNK
-    copies = devices // chunks
+    outers = devices // INNER
     me = lax.axis_index("lon")
     right, left = lax.rem(me + 1, devices), lax.rem(me + devices - 1, devices)
-    mine, which = me // copies, lax.rem(me, copies)
+    group_id, mine = me // INNER, lax.rem(me, INNER)
     weights = latitude_weights(rows)
     scale = 1.0 / (columns * devices * sum(weights))
 
@@ -156,51 +158,75 @@
         for copy in halo_copies(t):
             copy.start()
 
+    def push(source, target, send, recv, device):
+        return pltpu.make_async_remote_copy(
+            src_ref=source, dst_ref=target, send_sem=send, recv_sem=recv, device_id={"lon": device}
+        )
+
     def scatter(t, target, source):
-        return pltpu.make_async_remote_copy(
-            src_ref=part.at[t, target // copies],
-            dst_ref=gathered.at[t, source],
-            send_sem=rs_send.at[t, target],
-            recv_sem=rs_recv.at[t, source],
-            device_id={"lon": target},
-        )
+        return push(
+            part.at[t, target],
+            gathered.at[t, source],
+            rs_send.at[t, target],
+            rs_recv.at[t, source],
+            group_id * INNER + target,
+        )
+
+    def across(t, target, source):
+        return push(
+            outer.at[t, source],
+            outer.at[t, source],
+            ex_send.at[t, target],
+            ex_recv.at[t, source],
+            target * INNER + mine,
+        )
+
+    def spread(t, target, source):
+        return push(
+            combined.at[t, source],
+            combined.at[t, source],
+            ag_send.at[t, target],
+            ag_recv.at[t, source],
+            group_id * INNER + target,
+        )
+
+    def inner_peer(offset):
+        return lax.rem(mine + offset, INNER)
+
+    def outer_peer(offset):
+        return lax.rem(group_id + offset, outers)
 
     def start_scatter(t):
-        part[t] = acc[...].reshape(chunks, CHUNK, width)
-
-        @pl.loop(1, devices)
-        def _(offset):
-            scatter(t, peer(offset), me).start()
-
-    def spread(t, target, source):
-        return pltpu.make_async_remote_copy(
-            src_ref=combined.at[t, source],
-            dst_ref=combined.at[t, source],
-            send_sem=ag_send.at[t, target],
-            recv_sem=ag_recv.at[t, source],
-            device_id={"lon": target * copies + which},
-        )
+        part[t] = acc[...].reshape(INNER, levels // INNER, width)
+        for offset in range(1, INNER):
+            scatter(t, inner_peer(offset), mine).start()
 
     def combine(t):
-        gathered[t, me] = part[t, mine]
-
-        @pl.loop(1, devices)
-        def _(offset):
-            scatter(t, peer(offset), peer(offset)).wait_recv()
-
+        gathered[t, mine] = part[t, mine]
+        for offset in range(1, INNER):
+            other = inner_peer(offset)
+            scatter(t, other, other).wait_recv()
         total = gathered[t, 0]
-        for source in range(1, devices):
+        for source in range(1, INNER):
             total = total + gathered[t, source]
+        outer[t, group_id] = total
+        for offset in range(1, outers):
+            across(t, outer_peer(offset), group_id).start()
+
+    def combine_outer(t):
+        for offset in range(1, outers):
+            other = outer_peer(offset)
+            across(t, other, other).wait_recv()
+        total = outer[t, 0]
+        for source in range(1, outers):
+            total = total + outer[t, source]
         combined[t, mine] = total * scale
-
-        @pl.loop(1, chunks)
-        def _(offset):
-            spread(t, lax.rem(mine + offset, chunks), mine).start()
+        for offset in range(1, INNER):
+            spread(t, inner_peer(offset), mine).start()
 
     def finish(t):
-        @pl.loop(1, chunks)
-        def _(offset):
-            other = lax.rem(mine + offset, chunks)
+        for offset in range(1, INNER):
+            other = inner_peer(offset)
             spread(t, other, other).wait_recv()
 
         profile = combined[t].reshape(levels, width)
@@ -212,13 +238,11 @@
         for k in range(tiles):
             profiles[t, pl.ds(k, SUB, stride=tiles), :] = tiled[k]
 
-        @pl.loop(1, devices)
-        def _(offset):
-            scatter(t, peer(offset), me).wait_send()
-
-        @pl.loop(1, chunks)
-        def _(offset):
-            spread(t, lax.rem(mine + offset, chunks), mine).wait_send()
+        for offset in range(1, INNER):
+            scatter(t, inner_peer(offset), mine).wait_send()
+            spread(t, inner_peer(offset), mine).wait_send()
+        for offset in range(1, outers):
+            across(t, outer_peer(offset), group_id).wait_send()
 
     def accumulate(fresh):
         for j in range(rows):
@@ -230,6 +254,8 @@
         acc[...] += added
 
     acc[...] = jnp.zeros_like(acc)
+    ext[0] = jnp.zeros_like(ext[0])
+    ext[columns + 1] = jnp.zeros_like(ext[0])
 
     @pl.loop(0, groups)
     def _(k):
@@ -259,12 +285,7 @@
         return jnp.maximum(x, -edge_bias[index : index + 1])
 
     def edges(t):
-        for copy in halo_copies(t):
-            copy.wait_recv()
-        ext[0] = halo[t, 0]
-        ext[columns + 1] = halo[t, 1]
-        both = jnp.concatenate([ext[0].reshape(area, width), ext[1].reshape(area, width)], axis=1)
-        carry[...] = lifted(dot(both, w_pair[0, :, width:]), 1).reshape(rows, levels, width)
+        carry[...] = jnp.zeros_like(carry)
 
         @pl.loop(0, groups)
         def _(group):
@@ -273,13 +294,27 @@
                 combine(t)
 
             for piece in range(COLS // PER_DOT):
-                edge_piece(group * COLS + piece * PER_DOT)
+                edge_piece(group * COLS + piece * PER_DOT, PER_DOT)
+
+        combine_outer(t)
+        for copy in halo_copies(t):
+            copy.wait_recv()
+        ext[0] = halo[t, 0]
+        ext[columns + 1] = halo[t, 1]
+
+        @pl.loop(0, 2)
+        def _(side):
+            base = side * (columns - 1)
+            before = ext[base].reshape(area, width)
+            both = jnp.concatenate([before, ext[base + 1].reshape(area, width)], axis=1)
+            west = lifted(dot(both, w_pair[0, :, width:]), 1)
+            carry[...] = west.reshape(rows, levels, width)
+            edge_piece(base, 1)
 
         for copy in halo_copies(t):
             copy.wait_send()
 
-    def edge_piece(base):
-        n = PER_DOT
+    def edge_piece(base, n):
         here = ext[pl.ds(base + 1, n)]
         flat = here.reshape(n * area, width)
         ahead = ext[pl.ds(base + 2, n)].reshape(n * area, width)
@@ -397,7 +432,8 @@
     devices = lax.axis_size("lon")
     tiles = levels // SUB
     groups = columns // COLS
-    chunks = levels // CHUNK
+    outers = devices // INNER
+    piece = (levels // INNER, width)
     vmem = pl.BlockSpec(memory_space=pltpu.VMEM)
     hbm = pl.BlockSpec(memory_space=pl.ANY)
     dma = pltpu.SemaphoreType.DMA
@@ -424,17 +460,20 @@
             pltpu.VMEM((2 * width, 2 * width), BF16),
             pltpu.VMEM((levels, width), F32),
             pltpu.VMEM((levels, width), F32),
-            pltpu.VMEM((STEPS, chunks, CHUNK, width), F32),
-            pltpu.VMEM((STEPS, devices, CHUNK, width), F32),
-            pltpu.VMEM((STEPS, chunks, CHUNK, width), F32),
+            pltpu.VMEM((STEPS, INNER, *piece), F32),
+            pltpu.VMEM((STEPS, INNER, *piece), F32),
+            pltpu.VMEM((STEPS, outers, *piece), F32),
+            pltpu.VMEM((STEPS, INNER, *piece), F32),
             dma((groups,)),
             dma((groups,)),
             dma((STEPS, 2)),
             dma((STEPS, 2)),
-            dma((STEPS, devices)),
-            dma((STEPS, devices)),
-            dma((STEPS, chunks)),
-            dma((STEPS, chunks)),
+            dma((STEPS, INNER)),
+            dma((STEPS, INNER)),
+            dma((STEPS, outers)),
+            dma((STEPS, outers)),
+            dma((STEPS, INNER)),
+            dma((STEPS, INNER)),
         ],
         compiler_params=pltpu.CompilerParams(
             collective_id=0, has_side_effects=True, vmem_limit_bytes=60 * 1024 * 1024

time: 74.8 us -> 67.5 us (0.902)
  Pallas kernels: 70.1 us -> 62.8 us
    pallas_call x1, Pallas kernels: 70.1 us -> 62.8 us  [body(): pl.pallas_call(functools.partial(kernel, devices), out_shape=(jax.ShapeDt...]
where the time goes in v1:
time: 67.5 us; the launch traced here: 67.3 us
  Pallas kernels  62.8 us (93%)
  local copies, waits for them, and re-layouts  3.88 us (6%)
    pallas_call x1, Pallas kernels, body(): pl.pallas_call(functools.partial(kernel, devices), out_shape=(jax.ShapeDt...  62.8 us
    unnamed x4, local copies, waits for them, and re-layouts  3.88 us

profile of v1, /device:TPU:0, one launch (start us, length us, event | category | flops | bytes accessed | tf_op | source)
XLA Modules:
  0.0 67.3 jit_solution(14683816467040112988)
XLA Ops:
  0.6 62.8 %shard_map.113 = (bf16[32,4,64,128]{3,2,1,0:T(8,128)(2,1)}, f32[4,64,128]{2,1,0:T(8,128)}) custom-call(bf16[32,4,64,128]{3,2,1,0:T(8,128)(2,1)} %state_in.1, bf16[128,128]{1,0:T(8,128)(2,1)} %self_weight.1, bf16[6,128,128]{2,1,0:T(8,128)(2,1)} %neighbour_weight.1, f32[6,128]{1,0:T(8,128)} %edge_bias.1, bf16[128,128]{1,0:T(8,128)(2,1)} %message_weight.1, ...), custom_call_target="tpu_custom_call" | custom-call | tf_op jit(solution)/shard_map/pallas_call | solution.py:440
  63.5 0.0 copy-start
  63.5 3.2 %copy.14 = bf16[32,4,64,128]{3,2,1,0:T(8,128)(2,1)} copy(bf16[32,4,64,128]{3,2,1,0:T(8,128)(2,1)} %get-tuple-element.4) | data formatting | bytes 4194304
  66.7 0.0 copy-done
  66.7 0.7 copy.15
Async XLA Ops:
  63.5 3.2 %copy-start = (f32[4,64,128]{2,1,0:T(8,128)S(1)}, f32[4,64,128]{2,1,0:T(8,128)}, u32[]{:S(2)}) copy-start(f32[4,64,128]{2,1,0:T(8,128)} %get-tuple-element.5) | copy-start | bytes 393220
